TPU v7x, 32 devices: a whole 2x2x4 slice. The times are simulated.
32 devices in a mesh: seq: 8 (over z, x), img: 2 (over y), fsdp: 2 (over core).
Axes of the slice: x: 2, y: 2, z: 4, core: 2. Of those that a mesh axis runs over, the one named last changes fastest.
Arguments:
- vision_feats: bfloat16 [2, 2304, 1024], P('img', ('seq', 'fsdp')), may hold values from -6 to 6
- ln_gain: float32 [1024], replicated, may hold values from 0.5 to 1.5
- ln_bias: float32 [1024], replicated, may hold values from -3 to 3
- w_in: bfloat16 [1024, 4096], P('fsdp', 'seq'), may hold values from -0.1875 to 0.1875
- b_in: float32 [4096], P('seq'), may hold values from -3 to 3
- w_out: bfloat16 [4096, 4096], P('seq', 'fsdp'), may hold values from -0.09375 to 0.09375
- lm_grad: bfloat16 [2, 4096, 4096], P('img', 'seq', 'fsdp'), may hold values from -0.079589844 to 0.079589844
- image_counts: int32 [2, 2], P('img'), may hold values from 1 to 3, as said below
- token_pos: int32 [2, 2304], P('img'), may hold values from 0 to 2047, as said below
Outputs:
- w_in_grad: float32 [1024, 4096], P(('img', 'fsdp'), 'seq')
- b_in_grad: float32 [4096], replicated
- w_out_grad: float32 [4096, 4096], P(('seq', 'img'), 'fsdp')
- b_out_grad: float32 [4096], replicated
- ln_gain_grad: float32 [1024], replicated
- ln_bias_grad: float32 [1024], replicated
Inputs may be any that keep to these rules, and one draw needn't show every extreme that they name: `image_counts`: in each group the 2 samples hold 4 images together, each sample one or more. `token_pos`: each image's 576 tokens take consecutive positions of its sample's sequence in order; a sample's images come in order without intersection, and images are numbered sample by sample as image_counts gives.
All inputs are finite; a program needn't handle non-finite values.
Results may differ from a plain program's by a relative error of at most 0.0047.
Values may be sent and summed in bfloat16 or wider, within the bound.
A program may use at most 128 MiB of HBM per device.

v0:
```python
import jax
import jax.numpy as jnp
from jax import lax
from jax.sharding import PartitionSpec as P

PATCH = 576
LEN = 2048


def gelu_parts(preact):
    cumul = 0.5 * (1.0 + lax.erf(preact * 0.7071067811865476))
    density = jnp.exp(-0.5 * preact * preact) * 0.3989422804014327
    return (preact * cumul, cumul + preact * density)


def contract(left, right, left_dim, right_dim):
    return lax.dot_general(
        left, right, (((left_dim,), (right_dim,)), ((), ())), preferred_element_type=jnp.float32
    )


def own_columns(matrix, img_count, fsdp_count, fsdp_index):
    rows = matrix.shape[0]
    block = matrix.shape[1] // (img_count * fsdp_count)
    shaped = matrix.reshape(rows, img_count, fsdp_count, block)
    taken = lax.dynamic_index_in_dim(shaped, fsdp_index, axis=2, keepdims=False)
    return taken.reshape(rows, img_count * block)


def place_columns(vector, img_count, fsdp_count, fsdp_index):
    block = vector.shape[0] // img_count
    holder = jnp.zeros((img_count, fsdp_count, block), jnp.float32)
    holder = lax.dynamic_update_slice(
        holder, vector.reshape(img_count, 1, block), (0, fsdp_index, 0)
    )
    return holder.reshape(img_count * fsdp_count * block)


def per_device(vision_feats, ln_gain, ln_bias, w_in, b_in, w_out, lm_grad, image_counts, token_pos):
    seq_count = lax.axis_size("seq")
    seq_index = lax.axis_index("seq")
    img_count = lax.axis_size("img")
    fsdp_count = lax.axis_size("fsdp")
    fsdp_index = lax.axis_index("fsdp")
    lm_block = lm_grad[0]
    block_rows = lm_block.shape[0]
    half_width = lm_block.shape[1]
    position_count = block_rows * seq_count
    counts = image_counts[0]
    positions = token_pos[0]
    row_count = positions.shape[0]
    image_index = jnp.arange(row_count, dtype=jnp.int32) // PATCH
    bounds = jnp.cumsum(counts)
    sample = jnp.sum((image_index[:, None] >= bounds[None, :]).astype(jnp.int32), axis=1)
    abs_pos = sample * LEN + positions
    marker = jnp.zeros((position_count,), jnp.float32).at[abs_pos].set(1.0)
    own_mask = lax.dynamic_slice_in_dim(marker, seq_index * block_rows, block_rows).astype(
        jnp.bfloat16
    )
    out_bias_half = jnp.dot(own_mask[None, :], lm_block, preferred_element_type=jnp.float32)[0]
    out_bias_full = lax.dynamic_update_slice_in_dim(
        jnp.zeros((half_width * fsdp_count,), jnp.float32),
        out_bias_half,
        fsdp_index * half_width,
        0,
    )
    w_in_full = lax.all_gather(w_in, "fsdp", axis=0, tiled=True)
    gathered = lax.all_gather(vision_feats[0], ("seq", "fsdp"), axis=0, tiled=True)
    values = gathered.astype(jnp.float32)
    row_mean = jnp.mean(values, axis=1, keepdims=True)
    centred = values - row_mean
    row_var = jnp.mean(centred * centred, axis=1, keepdims=True)
    normed = centred * lax.rsqrt(row_var + 1e-05)
    normed_in = (normed * ln_gain + ln_bias).astype(jnp.bfloat16)
    preact = jnp.dot(normed_in, w_in_full, preferred_element_type=jnp.float32) + b_in
    activ, slope = gelu_parts(preact)
    hidden = activ.astype(jnp.bfloat16)
    hidden_width = hidden.shape[1]
    whole_grad = lax.all_gather(lm_block, "seq", axis=0, tiled=True)
    picked = whole_grad[abs_pos]
    hidden_part = contract(picked, w_out, 1, 1)
    w_out_part = contract(hidden, picked, 0, 0)
    hidden_grad = lax.psum(hidden_part, "fsdp")
    preact_grad = (hidden_grad * slope).astype(jnp.bfloat16)
    own_normed_in = own_columns(normed_in, img_count, fsdp_count, fsdp_index)
    own_normed = own_columns(normed, img_count, fsdp_count, fsdp_index)
    own_w_in = own_columns(w_in_full.T, img_count, fsdp_count, fsdp_index)
    w_in_part = contract(own_normed_in, preact_grad, 0, 0)
    half_rows = row_count // fsdp_count
    own_rows = lax.dynamic_slice_in_dim(preact_grad, fsdp_index * half_rows, half_rows, 0)
    b_in_part = jnp.sum(own_rows, axis=0, dtype=jnp.float32)
    normed_grad = contract(preact_grad, own_w_in, 1, 0)
    gain_part = place_columns(
        jnp.sum(normed_grad * own_normed, axis=0), img_count, fsdp_count, fsdp_index
    )
    bias_part = place_columns(jnp.sum(normed_grad, axis=0), img_count, fsdp_count, fsdp_index)
    w_in_grad, w_out_grad = (
        lax.psum_scatter(w_in_part, "img", scatter_dimension=0, tiled=True),
        lax.psum_scatter(w_out_part, "img", scatter_dimension=0, tiled=True),
    )
    hidden_full = lax.dynamic_update_slice_in_dim(
        jnp.zeros((hidden_width * seq_count,), jnp.float32), b_in_part, seq_index * hidden_width, 0
    )
    gain_grad, bias_grad, b_in_grad, b_out_grad = lax.psum(
        (gain_part, bias_part, hidden_full, out_bias_full), ("seq", "img", "fsdp")
    )
    return (w_in_grad, b_in_grad, w_out_grad, b_out_grad, gain_grad, bias_grad)


def solution(mesh):
    return jax.shard_map(
        per_device,
        mesh=mesh,
        in_specs=(
            P("img", ("seq", "fsdp"), None),
            P(),
            P(),
            P("fsdp", "seq"),
            P("seq"),
            P("seq", "fsdp"),
            P("img", "seq", "fsdp"),
            P("img", None),
            P("img", None),
        ),
        out_specs=(P(("img", "fsdp"), "seq"), P(), P(("seq", "img"), "fsdp"), P(), P(), P()),
        check_vma=False,
    )
```

profile of v0, /device:TPU:0, one launch (start us, length us, event | category | flops | bytes accessed | tf_op | source)
XLA Modules:
  0.0 437.1 jit_solution(6674310867122269369)
XLA Ops:
  7.2 0.0 copy-start
  7.2 0.0 all-gather.10.cloned.1.call-start
  7.2 0.7 all-gather.10.cloned.1.call-update
  7.9 0.0 all-gather.8.cloned.1.call-start
  8.0 0.7 all-gather.8.cloned.1.call-update
  8.7 0.0 all-gather.6.cloned.1.call-start
  8.7 0.7 all-gather.6.cloned.1.call-update
  9.4 0.0 all-reduce.3.cloned.1.call-start
  9.5 0.8 reduce-window.8
  10.3 0.1 fusion.13
  10.4 0.7 fusion.17
  11.2 229.0 %all-gather.10.cloned.1.call-done = bf16[1,4096,2048]{2,1,0:T(8,128)(2,1)} async-done(((bf16[1,512,2048]{2,1,0:T(8,128)(2,1)}), bf16[1,4096,2048]{2,1,0:T(8,128)(2,1)}) %all-gather.10.cloned.1.call-update) | async-done | bytes 16777232 | tf_op jit(solution)/shard_map/all_gather | solution.py:79
  240.2 26.3 %gather_fusion = bf16[2304,2048]{1,0:T(8,128)(2,1)} fusion(bf16[4096,2048]{1,0:T(8,128)(2,1)} %bitcast.48, s32[3072]{0:T(1024)S(1)} %pad_clamp_fusion), kind=kCustom, calls=%fused_computation | custom fusion | bytes 18883584 | tf_op jit(solution)/shard_map/gather | solution.py:80
  266.5 0.0 copy-done
  266.5 11.0 %fusion.21 = f32[2304,512]{1,0:T(8,128)} fusion(bf16[2304,2048]{1,0:T(8,128)(2,1)} %gather_fusion, bf16[512,2048]{1,0:T(8,128)(2,1)S(1)} %copy-done), kind=kOutput, calls=%fused_computation.47 | convolution fusion | flops 4831838208 | bytes 16252928 | tf_op jit(solution)/shard_map/dot_general | solution.py:17
  277.5 0.0 all-reduce.3.cloned.1.call-update
  277.5 0.2 reduce-scatter.3.cloned.1.call-start
  277.8 16.0 %all-gather.8.cloned.1.call-done = bf16[1,2304,1024]{2,1,0:T(8,128)(2,1)} async-done(((bf16[1,144,1024]{2,1,0:T(8,128)(2,1)}), bf16[1,2304,1024]{2,1,0:T(8,128)(2,1)}) %all-gather.8.cloned.1.call-update) | async-done | bytes 4718608 | tf_op jit(solution)/shard_map/all_gather | solution.py:68
  293.8 6.8 %copy.21 = bf16[1,2304,1024]{1,2,0:T(8,128)(2,1)} copy(bf16[1,2304,1024]{2,1,0:T(8,128)(2,1)} %all-gather.8.cloned.1.call-done) | data formatting | bytes 9437184 | tf_op jit(solution)/shard_map/all_gather | solution.py:68
  300.6 3.4 convert_reduce_fusion
  303.9 0.6 copy-done.2
  304.5 1.3 fusion.3
  305.8 0.0 copy-done.7
  305.8 0.0 copy-done.8
  305.8 4.7 %fusion.1 = (f32[2304,1024]{0,1:T(8,128)}, bf16[2304,1024]{0,1:T(8,128)(2,1)S(1)}) fusion(bf16[1,2304,1024]{1,2,0:T(8,128)(2,1)S(1)} %copy-done.2, f32[2304]{0:T(1024)S(1)} %add_rsqrt_fusion, f32[2304]{0:T(1024)S(1)} %broadcast_multiply_fusion.1, f32[1024]{0:T(1024)S(1)} %copy-done.7, f32[1024]{0:T(1024)S(1)} %copy-done.8), kind=kLoop, calls=%fused_computation.5 | loop fusion | flops 14155776 | bytes 18900992 | tf_op jit(solution)/shard_map/mul | solution.py:73
  310.5 2.3 copy-done.3
  312.8 1.6 constant_dynamic-slice_fusion.2
  314.4 21.0 %all-reduce.3.cloned.1.call-done = f32[2304,512]{1,0:T(8,128)} async-done(((f32[2304,512]{1,0:T(8,128)}), f32[2304,512]{1,0:T(8,128)}) %all-reduce.3.cloned.1.call-update) | async-done | bytes 4718608 | tf_op jit(solution)/shard_map/psum | solution.py:83
  335.4 0.0 copy-done.9
  335.4 8.7 %fusion.9 = (bf16[2304,512]{1,0:T(8,128)(2,1)S(1)}, f32[2304,512]{1,0:T(8,128)}) fusion(f32[2304,512]{1,0:T(8,128)} %all-reduce.3.cloned.1.call-done, f32[512]{0:T(512)S(1)} %copy-done.9, bf16[2304,1024]{0,1:T(8,128)(2,1)} %copy-done.3, bf16[1024,512]{1,0:T(8,128)(2,1)} %all-gather.6.cloned.1.call-done), kind=kOutput, calls=%fused_computation.16 | convolution fusion | flops 2428895232 | bytes 17565696 | tf_op jit(solution)/shard_map/dot_general | solution.py:75
  344.1 1.4 copy-done.6
  345.5 2.4 fusion.22
  347.8 0.0 reduce-scatter.3.cloned.1.call-update
  347.9 0.0 reduce-scatter.5.cloned.1.call-start
  347.9 0.0 copy-start.4
  347.9 11.1 %fusion.10 = f32[512,2048]{1,0:T(8,128)} fusion(bf16[2304,2048]{1,0:T(8,128)(2,1)} %gather_fusion, f32[2304,512]{1,0:T(8,128)} %get-tuple-element.15), kind=kOutput, calls=%fused_computation.20 | convolution fusion | flops 4837736448 | bytes 18350080 | tf_op jit(solution)/shard_map/dot_general | solution.py:17
  359.1 0.0 reduce-scatter.5.cloned.1.call-update
  359.1 9.2 %scatter_custom_fusion = f32[4096]{0:T(1024)S(1)} fusion(s32[2304]{0:T(1024)S(1)} %fusion.17, f32[2304]{0:T(1024)S(1)} %broadcast.81, f32[]{:T(128)} %constant.21.clone.1), kind=kCustom, calls=%fused_computation.38 | custom fusion | bytes 16388 | tf_op jit(solution)/shard_map/scatter | solution.py:56
  368.3 0.1 dynamic_slice.28
  368.4 0.4 fusion.11
  368.8 0.3 dynamic_update_slice.13
  369.1 1.1 constant_dynamic-slice_fusion.1
  370.1 4.9 %constant_dynamic-slice_fusion = f32[2304,2,1,256]{0,3,2,1:T(8,128)} fusion(f32[2304,2,2,256]{0,3,2,1:T(8,128)} %bitcast.49, s32[]{:T(128)S(6)} %select_n.40), kind=kLoop, calls=%fused_computation.43 | loop fusion | bytes 9437188 | tf_op jit(solution)/shard_map/jit(dynamic_index_in_dim)/dynamic_slice | solution.py:26
  375.0 6.1 %copy.24 = f32[2304,512]{1,0:T(8,128)} copy(f32[2304,512]{0,1:T(8,128)} %bitcast.50) | data formatting | bytes 9437184 | tf_op jit(solution)/shard_map/reshape | solution.py:27
  381.2 4.6 %fusion.20 = (f32[512]{0:T(512)S(1)}, f32[512]{0:T(512)S(1)}) fusion(f32[2304,512]{1,0:T(8,128)} %copy.24, bf16[2304,512]{1,0:T(8,128)(2,1)} %copy-done.6, bf16[512,512]{0,1:T(8,128)(2,1)S(1)} %bitcast.53), kind=kOutput, calls=%fused_computation.46 | convolution fusion | flops 1211497472 | bytes 7606272 | tf_op jit(solution)/shard_map/dot_general | solution.py:17
  385.9 1.5 convert_reduce_fusion.1
  387.4 0.3 dynamic_update_slice.12
  387.7 42.6 %all-reduce = (f32[4096]{0:T(1024)}, f32[4096]{0:T(1024)}, f32[1024]{0:T(1024)}, f32[1024]{0:T(1024)}) all-reduce(f32[4096]{0:T(1024)S(1)} %dynamic_update_slice.12, f32[4096]{0:T(1024)S(1)} %dynamic_update_slice.13, f32[1024]{0:T(1024)S(1)} %bitcast.57, ...), channel_id=1, replica_groups=mesh['seq'=8,'img'=2,'fsdp'=2] {'seq','img','fsdp'}, use_global_device_ids=true, to_apply=%region_7.8 | all-reduce | flops 10240 | bytes 81920 | tf_op jit(solution)/shard_map/psum | solution.py:104
  (29 shorter events, 0.2 us)
Async XLA Ops:
  7.2 259.3 %copy-start = (bf16[512,2048]{1,0:T(8,128)(2,1)S(1)}, bf16[512,2048]{1,0:T(8,128)(2,1)}, u32[]{:S(2)}) copy-start(bf16[512,2048]{1,0:T(8,128)(2,1)} %param.14) | copy-start | bytes 6291460
  7.2 233.0 %all-gather.10.cloned.1.call-start = ((), (), s32[]{:S(2)}) async-start(), calls=%async_computation.7 | async-start | bytes 18874368 | tf_op jit(solution)/shard_map/all_gather | solution.py:79
  7.9 285.9 %all-gather.8.cloned.1.call-start = ((), (), s32[]{:S(2)}) async-start(), calls=%async_computation.6 | async-start | bytes 5013504 | tf_op jit(solution)/shard_map/all_gather | solution.py:68
  8.7 305.7 %all-gather.6.cloned.1.call-start = ((), (), s32[]{:S(2)}) async-start(), calls=%async_computation.3 | async-start | bytes 1572864 | tf_op jit(solution)/shard_map/all_gather | solution.py:67
  9.4 326.0 %all-reduce.3.cloned.1.call-start = ((), (), s32[]{:S(2)}) async-start(), calls=%async_computation.2 | async-start | bytes 9437184 | tf_op jit(solution)/shard_map/psum | solution.py:83
  277.5 152.7 %reduce-scatter.3.cloned.1.call-start = ((), (), s32[]{:S(2)}) async-start(), calls=%async_computation.4 | async-start | bytes 1572864 | tf_op jit(solution)/shard_map/reduce_scatter | solution.py:98
  300.6 4.0 copy-start.2
  300.6 5.3 %copy-start.7 = (f32[1024]{0:T(1024)S(1)}, f32[1024]{0:T(1024)}, u32[]{:S(2)}) copy-start(f32[1024]{0:T(1024)} %param.11) | copy-start | bytes 12292
  300.6 5.3 %copy-start.8 = (f32[1024]{0:T(1024)S(1)}, f32[1024]{0:T(1024)}, u32[]{:S(2)}) copy-start(f32[1024]{0:T(1024)} %param.10) | copy-start | bytes 12292
  310.5 2.3 copy-start.3
  310.5 24.8 %copy-start.9 = (f32[512]{0:T(512)S(1)}, f32[512]{0:T(512)}, u32[]{:S(2)}) copy-start(f32[512]{0:T(512)} %param.13) | copy-start | bytes 6148
  335.4 10.1 %copy-start.5 = (bf16[2304,2,1,256]{0,3,2,1:T(8,128)(2,1)S(1)}, bf16[2304,2,1,256]{0,3,2,1:T(8,128)(2,1)}, u32[]{:S(2)}) copy-start(bf16[2304,2,1,256]{0,3,2,1:T(8,128)(2,1)} %constant_dynamic-slice_fusion.2) | copy-start | bytes 7077892
  344.1 1.4 copy-start.6
  347.9 82.4 %reduce-scatter.5.cloned.1.call-start = ((), (), s32[]{:S(2)}) async-start(), calls=%async_computation.5 | async-start | bytes 6291456 | tf_op jit(solution)/shard_map/reduce_scatter | solution.py:99
  347.9 20.5 %copy-start.4 = (bf16[1,512,2048]{2,1,0:T(8,128)(2,1)S(1)}, bf16[1,512,2048]{2,1,0:T(8,128)(2,1)}, u32[]{:S(2)}) copy-start(bf16[1,512,2048]{2,1,0:T(8,128)(2,1)} %param.15) | copy-start | bytes 6291460
  381.2 49.1 %copy-start.1 = (bf16[512,2048]{1,0:T(8,128)(2,1)S(1)}, bf16[512,2048]{1,0:T(8,128)(2,1)}, u32[]{:S(2)}) copy-start(bf16[512,2048]{1,0:T(8,128)(2,1)} %param.14) | copy-start | bytes 6291460
Sparse Core Ops, SparseCore 0:
  10.1 229.9 all-gather.9
  242.4 51.2 all-gather.7
  295.3 7.5 all-gather.5
  305.3 30.0 all-reduce.2
  348.0 21.5 reduce-scatter.2
  372.3 55.2 reduce-scatter.4
where the time goes:
time: 438 us; the launch traced here: 437 us
  waiting for transfers between devices  268 us (61%)
  local copies, waits for them, and re-layouts  61 us (14%)
  blocking collectives  42.6 us (10%)
  matrix products  38.2 us (9%)
  between operations  14.2 us (3%)
  other arithmetic  12.6 us (3%)
    all_gather x1, waiting for transfers between devices, per_device(): whole_grad = lax.all_gather(lm_block, 'seq', axis=0, tiled=True)  229 us
    psum x1, blocking collectives, per_device(): lax.psum((gain_part, bias_part, hidden_full, out_bias_full), ('seq', 'img...  42.6 us
    dot_general x4, matrix products, contract(): lax.dot_general(left, right, (((left_dim,), (right_dim,)), ((), ())), pre...  29.2 us
    gather x1, local copies, waits for them, and re-layouts, per_device(): picked = whole_grad[abs_pos]  26.3 us
    psum x1, waiting for transfers between devices, per_device(): hidden_grad = lax.psum(hidden_part, 'fsdp')  21 us
    all_gather x1, waiting for transfers between devices, per_device(): lax.all_gather(vision_feats[0], ('seq', 'fsdp'), axis=0, tiled=True)  16 us
    scatter x1, local copies, waits for them, and re-layouts, per_device(): marker = jnp.zeros((position_count,), jnp.float32).at[abs_pos].set(1.0)  9.21 us
  transfers between devices with their start and end apart: 6, of which 3 were waited for; matrix products, arithmetic and copies ran while one was open for 22% of the time, Pallas kernels for 0%

commit v1 on v0

--- a/solution.py
+++ b/solution.py
@@ -101,8 +101,14 @@
     hidden_full = lax.dynamic_update_slice_in_dim(
         jnp.zeros((hidden_width * seq_count,), jnp.float32), b_in_part, seq_index * hidden_width, 0
     )
-    gain_grad, bias_grad, b_in_grad, b_out_grad = lax.psum(
-        (gain_part, bias_part, hidden_full, out_bias_full), ("seq", "img", "fsdp")
+
+    def _use_blocks(base_x):
+        for dev_j in (("img", "fsdp"), "seq"):
+            base_x = lax.psum(base_x, dev_j)
+        return base_x
+
+    gain_grad, bias_grad, b_in_grad, b_out_grad = _use_blocks(
+        (gain_part, bias_part, hidden_full, out_bias_full)
     )
     return (w_in_grad, b_in_grad, w_out_grad, b_out_grad, gain_grad, bias_grad)
 

time: 438 us -> 447 us (1.021)
  blocking collectives: 42.6 us -> 52.3 us
    psum x1 -> x2, blocking collectives: 42.6 us -> 52.3 us  [_use_blocks(): base_x = lax.psum(base_x, dev_j)]
where the time goes in v1:
time: 447 us
  waiting for transfers between devices  268 us (60%)
  local copies, waits for them, and re-layouts  61 us (14%)
  blocking collectives  52.3 us (12%)
  matrix products  38.2 us (9%)
  between operations  14.2 us (3%)
  other arithmetic  12.6 us (3%)
    all_gather x1, waiting for transfers between devices, per_device(): whole_grad = lax.all_gather(lm_block, 'seq', axis=0, tiled=True)  229 us
    psum x2, blocking collectives, _use_blocks(): base_x = lax.psum(base_x, dev_j)  52.3 us
    dot_general x4, matrix products, contract(): lax.dot_general(left, right, (((left_dim,), (right_dim,)), ((), ())), pre...  29.2 us
    gather x1, local copies, waits for them, and re-layouts, per_device(): picked = whole_grad[abs_pos]  26.3 us
    psum x1, waiting for transfers between devices, per_device(): hidden_grad = lax.psum(hidden_part, 'fsdp')  21 us
    all_gather x1, waiting for transfers between devices, per_device(): lax.all_gather(vision_feats[0], ('seq', 'fsdp'), axis=0, tiled=True)  16 us
    scatter x1, local copies, waits for them, and re-layouts, per_device(): marker = jnp.zeros((position_count,), jnp.float32).at[abs_pos].set(1.0)  9.21 us
  transfers between devices with their start and end apart: 6, of which 3 were waited for; matrix products, arithmetic and copies ran while one was open for 22% of the time, Pallas kernels for 0%

profile of v1, /device:TPU:0, one launch (start us, length us, event | category | flops | bytes accessed | tf_op | source)
XLA Modules:
  0.0 446.9 jit_solution(11221132149485244769)
XLA Ops:
  7.2 0.0 copy-start
  7.2 0.0 all-gather.10.cloned.1.call-start
  7.2 0.7 all-gather.10.cloned.1.call-update
  7.9 0.0 all-gather.8.cloned.1.call-start
  8.0 0.7 all-gather.8.cloned.1.call-update
  8.7 0.0 all-gather.6.cloned.1.call-start
  8.7 0.7 all-gather.6.cloned.1.call-update
  9.4 0.0 all-reduce.4.cloned.1.call-start
  9.5 0.8 reduce-window.8
  10.3 0.1 fusion.13
  10.4 0.7 fusion.17
  11.2 229.0 %all-gather.10.cloned.1.call-done = bf16[1,4096,2048]{2,1,0:T(8,128)(2,1)} async-done(((bf16[1,512,2048]{2,1,0:T(8,128)(2,1)}), bf16[1,4096,2048]{2,1,0:T(8,128)(2,1)}) %all-gather.10.cloned.1.call-update) | async-done | bytes 16777232 | tf_op jit(solution)/shard_map/all_gather | solution.py:79
  240.2 26.3 %gather_fusion = bf16[2304,2048]{1,0:T(8,128)(2,1)} fusion(bf16[4096,2048]{1,0:T(8,128)(2,1)} %bitcast.48, s32[3072]{0:T(1024)S(1)} %pad_clamp_fusion), kind=kCustom, calls=%fused_computation | custom fusion | bytes 18883584 | tf_op jit(solution)/shard_map/gather | solution.py:80
  266.5 0.0 copy-done
  266.5 11.0 %fusion.21 = f32[2304,512]{1,0:T(8,128)} fusion(bf16[2304,2048]{1,0:T(8,128)(2,1)} %gather_fusion, bf16[512,2048]{1,0:T(8,128)(2,1)S(1)} %copy-done), kind=kOutput, calls=%fused_computation.47 | convolution fusion | flops 4831838208 | bytes 16252928 | tf_op jit(solution)/shard_map/dot_general | solution.py:17
  277.5 0.0 all-reduce.4.cloned.1.call-update
  277.5 0.2 reduce-scatter.3.cloned.1.call-start
  277.8 16.0 %all-gather.8.cloned.1.call-done = bf16[1,2304,1024]{2,1,0:T(8,128)(2,1)} async-done(((bf16[1,144,1024]{2,1,0:T(8,128)(2,1)}), bf16[1,2304,1024]{2,1,0:T(8,128)(2,1)}) %all-gather.8.cloned.1.call-update) | async-done | bytes 4718608 | tf_op jit(solution)/shard_map/all_gather | solution.py:68
  293.8 6.8 %copy.21 = bf16[1,2304,1024]{1,2,0:T(8,128)(2,1)} copy(bf16[1,2304,1024]{2,1,0:T(8,128)(2,1)} %all-gather.8.cloned.1.call-done) | data formatting | bytes 9437184 | tf_op jit(solution)/shard_map/all_gather | solution.py:68
  300.6 3.4 convert_reduce_fusion
  303.9 0.6 copy-done.2
  304.5 1.3 fusion.3
  305.8 0.0 copy-done.7
  305.8 4.7 %fusion.1 = (f32[2304,1024]{0,1:T(8,128)}, bf16[2304,1024]{0,1:T(8,128)(2,1)S(1)}) fusion(bf16[1,2304,1024]{1,2,0:T(8,128)(2,1)S(1)} %copy-done.2, f32[2304]{0:T(1024)S(1)} %add_rsqrt_fusion, f32[2304]{0:T(1024)S(1)} %broadcast_multiply_fusion.1, f32[1024]{0:T(1024)S(1)} %copy-done.7, f32[1024]{0:T(1024)S(1)} %copy-done.8), kind=kLoop, calls=%fused_computation.5 | loop fusion | flops 14155776 | bytes 18900992 | tf_op jit(solution)/shard_map/mul | solution.py:73
  310.5 2.3 copy-done.3
  312.8 1.6 constant_dynamic-slice_fusion.2
  314.4 21.0 %all-reduce.4.cloned.1.call-done = f32[2304,512]{1,0:T(8,128)} async-done(((f32[2304,512]{1,0:T(8,128)}), f32[2304,512]{1,0:T(8,128)}) %all-reduce.4.cloned.1.call-update) | async-done | bytes 4718608 | tf_op jit(solution)/shard_map/psum | solution.py:83
  335.4 8.7 %fusion.9 = (bf16[2304,512]{1,0:T(8,128)(2,1)S(1)}, f32[2304,512]{1,0:T(8,128)}) fusion(f32[2304,512]{1,0:T(8,128)} %all-reduce.4.cloned.1.call-done, f32[512]{0:T(512)S(1)} %copy-done.9, bf16[2304,1024]{0,1:T(8,128)(2,1)} %copy-done.3, bf16[1024,512]{1,0:T(8,128)(2,1)} %all-gather.6.cloned.1.call-done), kind=kOutput, calls=%fused_computation.16 | convolution fusion | flops 2428895232 | bytes 17565696 | tf_op jit(solution)/shard_map/dot_general | solution.py:75
  344.1 1.4 copy-done.6
  345.5 2.4 fusion.22
  347.8 0.0 reduce-scatter.3.cloned.1.call-update
  347.9 0.0 reduce-scatter.5.cloned.1.call-start
  347.9 0.0 copy-start.4
  347.9 11.1 %fusion.10 = f32[512,2048]{1,0:T(8,128)} fusion(bf16[2304,2048]{1,0:T(8,128)(2,1)} %gather_fusion, f32[2304,512]{1,0:T(8,128)} %get-tuple-element.19), kind=kOutput, calls=%fused_computation.20 | convolution fusion | flops 4837736448 | bytes 18350080 | tf_op jit(solution)/shard_map/dot_general | solution.py:17
  359.1 0.0 reduce-scatter.5.cloned.1.call-update
  359.1 9.2 %scatter_custom_fusion = f32[4096]{0:T(1024)S(1)} fusion(s32[2304]{0:T(1024)S(1)} %fusion.17, f32[2304]{0:T(1024)S(1)} %broadcast.81, f32[]{:T(128)} %constant.21.clone.1), kind=kCustom, calls=%fused_computation.38 | custom fusion | bytes 16388 | tf_op jit(solution)/shard_map/scatter | solution.py:56
  368.3 0.1 dynamic_slice.28
  368.4 0.4 fusion.11
  368.8 0.3 dynamic_update_slice.13
  369.1 1.1 constant_dynamic-slice_fusion.1
  370.1 4.9 %constant_dynamic-slice_fusion = f32[2304,2,1,256]{0,3,2,1:T(8,128)} fusion(f32[2304,2,2,256]{0,3,2,1:T(8,128)} %bitcast.49, s32[]{:T(128)S(6)} %select_n.40), kind=kLoop, calls=%fused_computation.43 | loop fusion | bytes 9437188 | tf_op jit(solution)/shard_map/jit(dynamic_index_in_dim)/dynamic_slice | solution.py:26
  375.0 6.1 %copy.24 = f32[2304,512]{1,0:T(8,128)} copy(f32[2304,512]{0,1:T(8,128)} %bitcast.50) | data formatting | bytes 9437184 | tf_op jit(solution)/shard_map/reshape | solution.py:27
  381.2 4.6 %fusion.20 = (f32[512]{0:T(512)S(1)}, f32[512]{0:T(512)S(1)}) fusion(f32[2304,512]{1,0:T(8,128)} %copy.24, bf16[2304,512]{1,0:T(8,128)(2,1)} %copy-done.6, bf16[512,512]{0,1:T(8,128)(2,1)S(1)} %bitcast.53), kind=kOutput, calls=%fused_computation.46 | convolution fusion | flops 1211497472 | bytes 7606272 | tf_op jit(solution)/shard_map/dot_general | solution.py:17
  385.9 1.5 convert_reduce_fusion.1
  387.4 0.3 dynamic_update_slice.12
  387.7 14.2 %all-reduce.1 = (f32[4096]{0:T(1024)S(1)}, f32[4096]{0:T(1024)S(1)}, f32[1024]{0:T(1024)S(1)}, f32[1024]{0:T(1024)S(1)}) all-reduce(f32[4096]{0:T(1024)S(1)} %dynamic_update_slice.12, f32[4096]{0:T(1024)S(1)} %dynamic_update_slice.13, f32[1024]{0:T(1024)S(1)} %bitcast.57, ...), channel_id=1, replica_groups=mesh['seq'=8,'img'=2,'fsdp'=2] {'img','fsdp'}, use_global_device_ids=true, to_apply=%region_7.8 | all-reduce | flops 10240 | bytes 81920 | tf_op jit(solution)/shard_map/psum | solution.py:107
  401.9 38.1 %all-reduce = (f32[4096]{0:T(1024)}, f32[4096]{0:T(1024)}, f32[1024]{0:T(1024)}, f32[1024]{0:T(1024)}) all-reduce(f32[4096]{0:T(1024)S(1)} %get-tuple-element.12, f32[4096]{0:T(1024)S(1)} %get-tuple-element.13, f32[1024]{0:T(1024)S(1)} %get-tuple-element.14, ...), channel_id=1, replica_groups=mesh['seq'=8,'img'=2,'fsdp'=2] {'seq'}, use_global_device_ids=true, to_apply=%region_8.9 | all-reduce | flops 10240 | bytes 81920 | tf_op jit(solution)/shard_map/psum | solution.py:107
  440.0 0.0 copy-done.1
  (30 shorter events, 0.2 us)
Async XLA Ops:
  7.2 259.3 %copy-start = (bf16[512,2048]{1,0:T(8,128)(2,1)S(1)}, bf16[512,2048]{1,0:T(8,128)(2,1)}, u32[]{:S(2)}) copy-start(bf16[512,2048]{1,0:T(8,128)(2,1)} %param.14) | copy-start | bytes 6291460
  7.2 233.0 %all-gather.10.cloned.1.call-start = ((), (), s32[]{:S(2)}) async-start(), calls=%async_computation.7 | async-start | bytes 18874368 | tf_op jit(solution)/shard_map/all_gather | solution.py:79
  7.9 285.9 %all-gather.8.cloned.1.call-start = ((), (), s32[]{:S(2)}) async-start(), calls=%async_computation.6 | async-start | bytes 5013504 | tf_op jit(solution)/shard_map/all_gather | solution.py:68
  8.7 305.7 %all-gather.6.cloned.1.call-start = ((), (), s32[]{:S(2)}) async-start(), calls=%async_computation.3 | async-start | bytes 1572864 | tf_op jit(solution)/shard_map/all_gather | solution.py:67
  9.4 326.0 %all-reduce.4.cloned.1.call-start = ((), (), s32[]{:S(2)}) async-start(), calls=%async_computation.2 | async-start | bytes 9437184 | tf_op jit(solution)/shard_map/psum | solution.py:83
  277.5 162.5 %reduce-scatter.3.cloned.1.call-start = ((), (), s32[]{:S(2)}) async-start(), calls=%async_computation.4 | async-start | bytes 1572864 | tf_op jit(solution)/shard_map/reduce_scatter | solution.py:98
  300.6 4.0 copy-start.2
  300.6 5.3 %copy-start.7 = (f32[1024]{0:T(1024)S(1)}, f32[1024]{0:T(1024)}, u32[]{:S(2)}) copy-start(f32[1024]{0:T(1024)} %param.11) | copy-start | bytes 12292
  300.6 5.3 %copy-start.8 = (f32[1024]{0:T(1024)S(1)}, f32[1024]{0:T(1024)}, u32[]{:S(2)}) copy-start(f32[1024]{0:T(1024)} %param.10) | copy-start | bytes 12292
  310.5 2.3 copy-start.3
  310.5 24.8 %copy-start.9 = (f32[512]{0:T(512)S(1)}, f32[512]{0:T(512)}, u32[]{:S(2)}) copy-start(f32[512]{0:T(512)} %param.13) | copy-start | bytes 6148
  335.4 10.1 %copy-start.5 = (bf16[2304,2,1,256]{0,3,2,1:T(8,128)(2,1)S(1)}, bf16[2304,2,1,256]{0,3,2,1:T(8,128)(2,1)}, u32[]{:S(2)}) copy-start(bf16[2304,2,1,256]{0,3,2,1:T(8,128)(2,1)} %constant_dynamic-slice_fusion.2) | copy-start | bytes 7077892
  344.1 1.4 copy-start.6
  347.9 92.2 %reduce-scatter.5.cloned.1.call-start = ((), (), s32[]{:S(2)}) async-start(), calls=%async_computation.5 | async-start | bytes 6291456 | tf_op jit(solution)/shard_map/reduce_scatter | solution.py:99
  347.9 20.5 %copy-start.4 = (bf16[1,512,2048]{2,1,0:T(8,128)(2,1)S(1)}, bf16[1,512,2048]{2,1,0:T(8,128)(2,1)}, u32[]{:S(2)}) copy-start(bf16[1,512,2048]{2,1,0:T(8,128)(2,1)} %param.15) | copy-start | bytes 6291460
  381.2 58.9 %copy-start.1 = (bf16[512,2048]{1,0:T(8,128)(2,1)S(1)}, bf16[512,2048]{1,0:T(8,128)(2,1)}, u32[]{:S(2)}) copy-start(bf16[512,2048]{1,0:T(8,128)(2,1)} %param.14) | copy-start | bytes 6291460
Sparse Core Ops, SparseCore 0:
  10.1 229.9 all-gather.9
  242.4 51.2 all-gather.7
  295.3 7.5 all-gather.5
  305.3 30.0 all-reduce.3
  348.0 21.5 reduce-scatter.2
  372.3 55.1 reduce-scatter.4
